TPU v7x, 32 devices: a whole 2x2x4 slice. The times are simulated.
32 devices in a mesh: tm: 2 (over core), stn: 4 (over z), chan: 4 (over y, x).
Axes of the slice: x: 2, y: 2, z: 4, core: 2. Of those that a mesh axis runs over, the one named last changes fastest.
Arguments:
- voltages: bfloat16 [2, 8, 512, 32, 2, 256], P(None, 'chan', 'stn', 'tm'), may hold values from -100 to 100
- fir_taps: float32 [16, 256], replicated, may hold values from -1.5 to 1.5
- station_map: int32 [512], P('stn'), may hold values from 0 to 31, as said below
- beam_index: int32 [512], P('stn'), may hold values from 0 to 15
- weight_table: bfloat16 [2, 16, 8, 8], P(None, None, 'chan'), may hold values from -1.5 to 1.5
Outputs:
- visibilities: float32 [2, 2, 8, 32, 32, 8, 2, 2, 256], P('tm', None, 'chan', 'stn')
Inputs may be any that keep to these rules, and one draw needn't show every extreme that they name: `station_map`: each station number names exactly 16 dishes; of the dishes g * 128 up to (g + 1) * 128 - 1, exactly 32 name a station of the block h * 8 up to (h + 1) * 8 - 1, for every g and h.
All inputs are finite; a program needn't handle non-finite values.
Results may differ from a plain program's by a relative error of at most 0.017.
Values may be sent and summed in bfloat16 or wider, within the bound.
A program may use at most 512 MiB of HBM per device.

v0:
```python
import jax
import jax.numpy as jnp
from jax import lax
from jax.sharding import PartitionSpec as P

STATIONS = 32
COARSE = 8
epsilon = 1e-06


def shifted(value, axis, steps):
    count = lax.axis_size(axis)
    first, last = (max(0, -steps), min(count, count - steps))
    return lax.ppermute(value, axis, [(source, source + steps) for source in range(first, last)])


def dft_tables(length):
    bin_index = jnp.arange(length, dtype=jnp.int32)
    phase_step = bin_index[:, None] * bin_index[None, :] % length
    angles = phase_step.astype(jnp.float32) * (2.0 * jnp.pi / length)
    return (jnp.cos(angles).astype(jnp.bfloat16), jnp.sin(angles).astype(jnp.bfloat16))


def power_terms(formed):
    values = formed.astype(jnp.float32)
    return jnp.sum(values * values, axis=(1, 3, 4, 6))


def normalise(formed, power_sum, denominator):
    inverse_rms = lax.rsqrt(power_sum / denominator + epsilon)
    return (formed.astype(jnp.float32) * inverse_rms[:, None, :, None, None, :, None]).astype(
        jnp.bfloat16
    )


def correlate(left_beams, right_beams, frames_dev):

    def product(first_part, second_part):
        return jnp.einsum(
            "sbcfpk,tbcfqk->cstbpqk", first_part, second_part, preferred_element_type=jnp.float32
        )

    left_re = left_beams[:, 0]
    left_im = left_beams[:, 1]
    right_re = right_beams[:, 0]
    right_im = right_beams[:, 1]
    vis_re = product(left_re, right_re) + product(left_im, right_im)
    vis_im = product(left_im, right_re) - product(left_re, right_im)
    return jnp.stack([vis_re, vis_im]) / frames_dev


def mixing_of(row_hot, weight_table):
    weights = jnp.einsum("dt,otcb->ocdb", row_hot, weight_table, preferred_element_type=jnp.float32)
    weight_re = weights[0]
    weight_im = weights[1]
    return jnp.stack([jnp.stack([weight_re, -weight_im]), jnp.stack([weight_im, weight_re])])


def per_device(voltages, fir_taps, station_map, beam_index, weight_table):
    components, coarse_dev, dishes_dev, frames_dev, polars, fine_bins = voltages.shape
    history = fir_taps.shape[0] - 1
    table_rows = weight_table.shape[1]
    cosine, sine_table = dft_tables(fine_bins)
    earlier = shifted(voltages[:, :, :, frames_dev - history :], "tm", 1)
    extended = jnp.concatenate([earlier, voltages], axis=3)
    filtered = jnp.zeros(voltages.shape, jnp.float32)
    for tap_index in range(history + 1):
        offset = history - tap_index
        filtered = filtered + fir_taps[tap_index] * extended[
            :, :, :, offset : offset + frames_dev
        ].astype(jnp.float32)
    filtered = filtered.astype(jnp.bfloat16)
    real_part = filtered[0].reshape(-1, fine_bins)
    imag_part = filtered[1].reshape(-1, fine_bins)
    spec_re = jnp.dot(real_part, cosine, preferred_element_type=jnp.float32) + jnp.dot(
        imag_part, sine_table, preferred_element_type=jnp.float32
    )
    spec_im = jnp.dot(imag_part, cosine, preferred_element_type=jnp.float32) - jnp.dot(
        real_part, sine_table, preferred_element_type=jnp.float32
    )
    spectra = jnp.stack([spec_re, spec_im]).reshape(voltages.shape).astype(jnp.bfloat16)
    denominator = COARSE * frames_dev * fine_bins
    own_count = STATIONS // lax.axis_size("stn")
    station_hot = (station_map[:, None] == jnp.arange(STATIONS, dtype=jnp.int32)[None, :]).astype(
        jnp.float32
    )
    table_hot = (beam_index[:, None] == jnp.arange(table_rows, dtype=jnp.int32)[None, :]).astype(
        jnp.bfloat16
    )
    mixing = mixing_of(table_hot, weight_table)
    steering = (station_hot[None, None, None, :, :, None] * mixing[:, :, :, :, None, :]).astype(
        jnp.bfloat16
    )
    full_sums = jnp.einsum(
        "oicdsb,icdfpk->sobcfpk", steering, spectra, preferred_element_type=jnp.float32
    )
    formed = lax.psum(full_sums.astype(jnp.bfloat16), "stn")
    power_sum = lax.psum(power_terms(formed), "chan")
    normed = normalise(formed, power_sum, denominator)
    own_rows = lax.dynamic_slice_in_dim(normed, lax.axis_index("stn") * own_count, own_count, 0)
    visibility = correlate(own_rows, normed, frames_dev)
    return visibility[None]


def solution(mesh):
    in_specs = (
        P(None, "chan", "stn", "tm", None, None),
        P(),
        P("stn"),
        P("stn"),
        P(None, None, "chan", None),
    )
    out_specs = P("tm", None, "chan", "stn", None, None, None, None, None)
    return jax.shard_map(
        per_device, mesh=mesh, in_specs=in_specs, out_specs=out_specs, check_vma=False
    )
```

profile of v0, /device:TPU:0, one launch (start us, length us, event | category | flops | bytes accessed | tf_op | source)
XLA Modules:
  0.0 1312.8 jit_solution(9741827098668168143)
XLA Ops:
  6.5 0.0 copy-start
  6.5 0.0 all-reduce.2.cloned.1.call-start
  6.5 0.0 slice-start
  6.5 6.9 slice.122
  13.5 5.5 collective-permute-start
  18.9 0.0 copy-done
  18.9 0.8 fusion.20
  19.7 0.0 slice-start.1
  19.8 0.8 fusion.19
  20.6 1.1 fusion.40
  21.6 6.4 collective-permute-done
  28.0 6.8 constant_dynamic-update-slice_fusion.1
  34.8 0.0 slice-done
  34.8 0.0 slice-done.1
  34.8 8.4 constant_dynamic-update-slice_fusion
  43.3 108.3 %add_convert_fusion = bf16[2,2,128,16,2,256]{5,4,3,2,1,0:T(2,128)(2,1)} fusion(bf16[2,2,128,16,2,256]{5,4,3,2,1,0:T(2,128)(2,1)S(1)} %bitcast.86, bf16[2,2,128,31,2,256]{5,4,3,2,1,0:T(2,128)(2,1)S(1)} %constant_dynamic-update-slice_fusion, f32[256]{0:T(256)S(1)} %bitcast.102, f32[256]{0:T(256)S(1)} %bitcast.103, f32[256]{0:T(256)S(1)} %bitcast.89, ...), kind=kLoop, calls=%fused_computation.8 | loop fusion | flops 201326592 | bytes 142622720 | tf_op jit(solution)/shard_map/convert_element_type | solution.py:72
  151.6 10.2 fusion.39
  161.8 7.2 reshape_squeeze.6
  168.9 7.2 reshape_squeeze.7
  176.1 0.0 copy-start.3
  176.1 4.5 fusion.17
  180.6 0.0 copy-done.3
  180.6 5.6 fusion.18
  186.2 4.2 fusion.4
  190.4 7.3 stack.35
  197.8 0.0 copy-start.2
  197.8 7.7 copy.19
  205.5 0.0 copy-done.2
  205.5 6.4 fusion.3
  211.9 7.2 stack.34
  219.1 5.6 copy.18
  224.7 10.1 fusion.2
  234.8 0.0 all-reduce.2.cloned.1.call-update
  234.9 564.4 %all-reduce.2.cloned.1.call-done = bf16[32,2,8,2,16,2,256]{6,0,2,1,5,4,3:T(8,128)(2,1)} async-done(((bf16[32,2,8,2,16,2,256]{6,0,2,1,5,4,3:T(8,128)(2,1)}), bf16[32,2,8,2,16,2,256]{6,0,2,1,5,4,3:T(8,128)(2,1)}) %all-reduce.2.cloned.1.call-update) | async-done | bytes 16777232 | tf_op jit(solution)/shard_map/psum | solution.py:97
  799.3 7.4 fusion
  806.7 10.0 psum.15
  816.7 12.7 fusion.1
  829.4 6.4 slice_bitcast_fusion
  835.8 2.0 dynamic-slice_bitcast_fusion.1
  837.8 22.6 %copy.36 = bf16[8,8,2,16,2,256,1]{3,0,4,6,5,1,2:T(8,128)(2,1)} copy(bf16[8,8,2,16,2,256,1]{5,0,1,4,3,2,6:T(8,128)(2,1)} %get-tuple-element.5) | data formatting | bytes 4194304 | tf_op jit(solution)/shard_map/squeeze | solution.py:43
  860.4 16.6 %copy.38 = bf16[8,8,2,16,2,256,1]{3,0,4,6,5,1,2:T(8,128)(2,1)} copy(bf16[8,8,2,16,2,256,1]{5,0,1,4,3,2,6:T(8,128)(2,1)S(1)} %get-tuple-element.6) | data formatting | bytes 4194304 | tf_op jit(solution)/shard_map/squeeze | solution.py:44
  877.0 44.4 %copy.37 = bf16[32,8,2,16,2,256,1]{0,3,6,4,5,1,2:T(8,128)(2,1)} copy(bf16[32,8,2,16,2,256,1]{5,0,1,4,3,2,6:T(8,128)(2,1)} %get-tuple-element.7) | data formatting | bytes 16777216 | tf_op jit(solution)/shard_map/squeeze | solution.py:46
  921.4 44.4 %copy.35 = bf16[32,8,2,16,2,256,1]{0,3,6,4,5,1,2:T(8,128)(2,1)} copy(bf16[32,8,2,16,2,256,1]{5,0,1,4,3,2,6:T(8,128)(2,1)} %get-tuple-element.8) | data formatting | bytes 16777216 | tf_op jit(solution)/shard_map/squeeze | solution.py:45
  965.8 39.2 %fusion.42 = f32[2,8,256,32,2,8,2]{3,5,6,4,2,1,0:T(8,128)} fusion(bf16[32,8,2,16,2,256,1]{0,3,6,4,5,1,2:T(8,128)(2,1)} %copy.35, bf16[8,8,2,16,2,256,1]{3,0,4,6,5,1,2:T(8,128)(2,1)} %copy.38), kind=kOutput, calls=%fused_computation.70 | convolution fusion | flops 134217728 | bytes 27262976 | tf_op jit(solution)/shard_map/sbcfpk,tbcfqk->cstbpqk/dot_general | solution.py:39
  1005.0 39.2 %fusion.41 = f32[2,8,256,32,2,8,2]{3,5,6,4,2,1,0:T(8,128)} fusion(bf16[32,8,2,16,2,256,1]{0,3,6,4,5,1,2:T(8,128)(2,1)} %copy.35, bf16[8,8,2,16,2,256,1]{3,0,4,6,5,1,2:T(8,128)(2,1)} %copy.36), kind=kOutput, calls=%fused_computation.69 | convolution fusion | flops 134217728 | bytes 27262976 | tf_op jit(solution)/shard_map/sbcfpk,tbcfqk->cstbpqk/dot_general | solution.py:39
  1044.2 60.2 %subtract_bitcast_fusion = f32[1,1,2,8,32,8,2,2,256]{4,3,6,7,8,5,2,1,0:T(8,128)} fusion(f32[2,8,256,32,2,8,2]{3,5,6,4,2,1,0:T(8,128)} %fusion.42, bf16[32,8,2,16,2,256,1]{0,3,6,4,5,1,2:T(8,128)(2,1)} %copy.37, bf16[8,8,2,16,2,256,1]{3,0,4,6,5,1,2:T(8,128)(2,1)} %copy.36), kind=kOutput, calls=%fused_computation | convolution fusion | flops 138412032 | bytes 44040192 | tf_op jit(solution)/shard_map/sbcfpk,tbcfqk->cstbpqk/dot_general | solution.py:39
  1104.4 34.7 %copy.30 = f32[1,1,2,8,32,8,2,2,256]{8,5,7,6,4,3,2,1,0:T(8,128)} copy(f32[1,1,2,8,32,8,2,2,256]{4,3,6,7,8,5,2,1,0:T(8,128)} %subtract_bitcast_fusion) | data formatting | bytes 33554432 | tf_op jit(solution)/shard_map/stack | solution.py:49
  1139.1 60.5 %add_bitcast_fusion = f32[1,1,2,8,32,8,2,2,256]{4,3,6,7,8,5,2,1,0:T(8,128)} fusion(f32[2,8,256,32,2,8,2]{3,5,6,4,2,1,0:T(8,128)} %fusion.41, bf16[32,8,2,16,2,256,1]{0,3,6,4,5,1,2:T(8,128)(2,1)} %copy.37, bf16[8,8,2,16,2,256,1]{3,0,4,6,5,1,2:T(8,128)(2,1)} %copy.38), kind=kOutput, calls=%fused_computation.1 | convolution fusion | flops 138412032 | bytes 44040192 | tf_op jit(solution)/shard_map/sbcfpk,tbcfqk->cstbpqk/dot_general | solution.py:39
  1199.5 34.8 %copy.29 = f32[1,1,2,8,32,8,2,2,256]{8,5,7,6,4,3,2,1,0:T(8,128)} copy(f32[1,1,2,8,32,8,2,2,256]{4,3,6,7,8,5,2,1,0:T(8,128)} %add_bitcast_fusion) | data formatting | bytes 33554432 | tf_op jit(solution)/shard_map/stack | solution.py:49
  1234.3 24.9 %maximum_multiply_fusion = f32[1,2,2,8,32,8,2,2,256]{8,5,7,6,4,3,2,1,0:T(8,128)} fusion(f32[1,1,2,8,32,8,2,2,256]{8,5,7,6,4,3,2,1,0:T(8,128)} %copy.30, f32[1,1,2,8,32,8,2,2,256]{8,5,7,6,4,3,2,1,0:T(8,128)} %copy.29), kind=kLoop, calls=%fused_computation.6 | loop fusion | flops 16777216 | bytes 67108864 | tf_op jit(solution)/shard_map/div | solution.py:49
  1259.2 0.0 copy-start.1
  1259.2 46.3 %copy.31 = f32[1,2,2,8,32,8,2,2,256]{8,7,6,5,4,3,2,1,0:T(2,128)} copy(f32[1,2,2,8,32,8,2,2,256]{8,5,7,6,4,3,2,1,0:T(8,128)} %maximum_multiply_fusion) | data formatting | bytes 67108864 | tf_op jit(solution)/shard_map/div | solution.py:49
  1305.5 0.0 copy-done.1
  (6 shorter events, 0.0 us)
Async XLA Ops:
  6.5 12.4 copy-start
  6.5 792.8 %all-reduce.2.cloned.1.call-start = ((), (), s32[]{:S(2)}) async-start(), calls=%async_computation | async-start | bytes 33554432 | tf_op jit(solution)/shard_map/psum | solution.py:97
  6.5 28.2 %slice-start = ((s8[8388608]{0:T(1024)(128)(4,1)}), s8[4194304]{0:T(1024)(128)(4,1)S(1)}, s32[]{:S(2)}) async-start(s8[8388608]{0:T(1024)(128)(4,1)} %bitcast.85), calls=%async_computation.1 | async-start | bytes 8388608
  13.5 14.6 %collective-permute-start = (bf16[2,2,128,15,2,256]{5,4,3,2,1,0:T(2,128)(2,1)S(1)}, bf16[2,2,128,15,2,256]{5,4,3,2,1,0:T(2,128)(2,1)}, u32[]{:S(2)}, u32[]{:S(2)}) collective-permute-start(bf16[2,2,128,15,2,256]{5,4,3,2,1,0:T(2,128)(2,1)S(1)} %slice.122), channel_id=1, source_target_pairs={{0,16},{1,17},{2,18},{3,19},{4,20},{5,21},{6,22},{7,23},{8,24},{9,... | collective-permute-start | bytes 23592968 | tf_op jit(solution)/shard_map/ppermute | solution.py:14
  19.7 15.1 %slice-start.1 = ((s8[8388608]{0:T(1024)(128)(4,1)}), s8[4194304]{0:T(1024)(128)(4,1)S(1)}, s32[]{:S(2)}) async-start(s8[8388608]{0:T(1024)(128)(4,1)} %bitcast.85), calls=%async_computation.2 | async-start | bytes 8388608
  176.1 4.5 copy-start.3
  197.8 7.7 copy-start.2
  1259.2 46.3 %copy-start.1 = (bf16[2,16,2,8]{1,3,2,0:T(8,128)(2,1)S(1)}, bf16[2,16,2,8]{1,3,2,0:T(8,128)(2,1)}, u32[]{:S(2)}) copy-start(bf16[2,16,2,8]{1,3,2,0:T(8,128)(2,1)} %param.9) | copy-start | bytes 3076
Sparse Core Ops, SparseCore 0:
  235.0 564.2 all-reduce.1
where the time goes:
time: 1320 us; the launch traced here: 1310 us
  waiting for transfers between devices  571 us (43%)
  local copies, waits for them, and re-layouts  328 us (25%)
  matrix products  231 us (18%)
  other arithmetic  154 us (12%)
  between operations  14 us (1%)
    psum x1, waiting for transfers between devices, per_device(): formed = lax.psum(full_sums.astype(jnp.bfloat16), 'stn')  564 us
    dot_general x4, matrix products, product(): jnp.einsum('sbcfpk,tbcfqk->cstbpqk', first_part, second_part, preferred_e...  199 us
    convert_element_type x1, other arithmetic, per_device(): filtered = filtered.astype(jnp.bfloat16)  108 us
    another operation x2, local copies, waits for them, and re-layouts, correlate(): return jnp.stack([vis_re, vis_im]) / frames_dev  69.5 us
    squeeze x2, local copies, waits for them, and re-layouts, correlate(): right_im = right_beams[:, 1]  50.9 us
    div x1, local copies, waits for them, and re-layouts, correlate(): return jnp.stack([vis_re, vis_im]) / frames_dev  46.3 us
    squeeze x1, local copies, waits for them, and re-layouts, correlate(): right_re = right_beams[:, 0]  44.4 us
    another operation x4, local copies, waits for them, and re-layouts, per_device(): jnp.stack([spec_re, spec_im]).reshape(voltages.shape).astype(jnp.bfloat16)  27.9 us
  transfers between devices with their start and end apart: 2, of which 2 were waited for; matrix products, arithmetic and copies ran while one was open for 0% of the time, Pallas kernels for 0%

commit v1 on v0

--- a/solution.py
+++ b/solution.py
@@ -94,7 +94,7 @@
     full_sums = jnp.einsum(
         "oicdsb,icdfpk->sobcfpk", steering, spectra, preferred_element_type=jnp.float32
     )
-    formed = lax.psum(full_sums.astype(jnp.bfloat16), "stn")
+    formed = jnp.sum(lax.all_gather(full_sums.astype(jnp.bfloat16), "stn"), axis=0)
     power_sum = lax.psum(power_terms(formed), "chan")
     normed = normalise(formed, power_sum, denominator)
     own_rows = lax.dynamic_slice_in_dim(normed, lax.axis_index("stn") * own_count, own_count, 0)

time: 1320 us -> 2280 us (1.73)
  waiting for transfers between devices: 571 us -> 1120 us
  matrix products: 231 us -> 416 us
  other arithmetic: 154 us -> 298 us
  local copies, waits for them, and re-layouts: 328 us -> 404 us
    all_gather x0 -> x1, waiting for transfers between devices: none -> 1110 us  [per_device(): lax.all_gather(full_sums.astype(jnp.bfloat16), 'stn')]
    psum x1 -> x0, waiting for transfers between devices: 564 us -> none  [per_device(): formed = lax.psum(full_sums.astype(jnp.bfloat16), 'stn')]
    reduce_sum x0 -> x1, local copies, waits for them, and re-layouts: none -> 213 us  [per_device(): jnp.sum(lax.all_gather(full_sums.astype(jnp.bfloat16), 'stn'), axis=0)]
    dot_general x4, matrix products: 199 us -> 384 us  [product(): jnp.einsum('sbcfpk,tbcfqk->cstbpqk', first_part, second_part, preferred_e...]
    squeeze x6 -> x0, local copies, waits for them, and re-layouts: 136 us -> none  [the longest x2 50.9 us: correlate(): right_im = right_beams[:, 1]]
    convert_element_type x1, other arithmetic: 12.7 us -> 88.3 us  [normalise(): (formed.astype(jnp.float32) * inverse_rms[:, None, :, None, None, :, None...]
    reduce_sum x1, other arithmetic: 7.38 us -> 44.7 us  [power_terms(): return jnp.sum(values * values, axis=(1, 3, 4, 6))]
    reduce_sum x0 -> x1, other arithmetic: none -> 30.8 us  [per_device(): jnp.sum(lax.all_gather(full_sums.astype(jnp.bfloat16), 'stn'), axis=0)]
where the time goes in v1:
time: 2280 us; the launch traced here: 2270 us
  waiting for transfers between devices  1120 us (49%)
  matrix products  416 us (18%)
  local copies, waits for them, and re-layouts  404 us (18%)
  other arithmetic  298 us (13%)
    all_gather x1, waiting for transfers between devices, per_device(): lax.all_gather(full_sums.astype(jnp.bfloat16), 'stn')  1110 us
    dot_general x4, matrix products, product(): jnp.einsum('sbcfpk,tbcfqk->cstbpqk', first_part, second_part, preferred_e...  384 us
    reduce_sum x1, local copies, waits for them, and re-layouts, per_device(): jnp.sum(lax.all_gather(full_sums.astype(jnp.bfloat16), 'stn'), axis=0)  213 us
    convert_element_type x1, other arithmetic, per_device(): filtered = filtered.astype(jnp.bfloat16)  108 us
    convert_element_type x1, other arithmetic, normalise(): (formed.astype(jnp.float32) * inverse_rms[:, None, :, None, None, :, None...  88.3 us
    another operation x2, local copies, waits for them, and re-layouts, correlate(): return jnp.stack([vis_re, vis_im]) / frames_dev  69.4 us
    div x1, local copies, waits for them, and re-layouts, correlate(): return jnp.stack([vis_re, vis_im]) / frames_dev  46.3 us
  transfers between devices with their start and end apart: 2, of which 2 were waited for; matrix products, arithmetic and copies ran while one was open for 0% of the time, Pallas kernels for 0%

profile of v1, /device:TPU:0, one launch (start us, length us, event | category | flops | bytes accessed | tf_op | source)
XLA Modules:
  0.0 2266.2 jit_solution(7291640760725465447)
XLA Ops:
  6.5 0.0 copy-start
  6.5 0.0 all-gather.3.cloned.1.call-start
  6.5 0.0 slice-start
  6.5 6.9 slice.122
  13.5 5.5 collective-permute-start
  18.9 0.0 copy-done
  18.9 0.8 fusion.24
  19.7 0.0 slice-start.1
  19.8 0.8 fusion.23
  20.6 1.1 fusion.48
  21.7 6.3 collective-permute-done
  28.0 6.8 constant_dynamic-update-slice_fusion.1
  34.8 0.0 slice-done
  34.8 0.0 slice-done.1
  34.8 8.4 constant_dynamic-update-slice_fusion
  43.3 108.3 %add_convert_fusion = bf16[2,2,128,16,2,256]{5,4,3,2,1,0:T(2,128)(2,1)} fusion(bf16[2,2,128,16,2,256]{5,4,3,2,1,0:T(2,128)(2,1)S(1)} %bitcast.123, bf16[2,2,128,31,2,256]{5,4,3,2,1,0:T(2,128)(2,1)S(1)} %constant_dynamic-update-slice_fusion, f32[256]{0:T(256)S(1)} %bitcast.139, f32[256]{0:T(256)S(1)} %bitcast.140, f32[256]{0:T(256)S(1)} %bitcast.126, ...), kind=kLoop, calls=%fused_computation.16 | loop fusion | flops 201326592 | bytes 142622720 | tf_op jit(solution)/shard_map/convert_element_type | solution.py:72
  151.6 10.2 fusion.47
  161.7 7.2 reshape_squeeze.6
  168.9 7.2 reshape_squeeze.7
  176.1 0.0 copy-start.3
  176.1 4.5 fusion.21
  180.6 0.0 copy-done.3
  180.6 5.6 fusion.22
  186.2 4.2 fusion.8
  190.4 7.4 stack.35
  197.8 0.0 copy-start.2
  197.8 7.8 copy.15
  205.5 0.0 copy-done.2
  205.5 6.4 fusion.7
  211.9 7.2 stack.34
  219.1 5.6 copy.14
  224.7 10.3 fusion.6
  235.1 0.0 all-gather.3.cloned.1.call-update
  235.1 1112.8 %all-gather.3.cloned.1.call-done = bf16[128,2,8,2,16,2,256]{6,0,2,1,5,4,3:T(8,128)(2,1)} async-done(((bf16[32,2,8,2,16,2,256]{6,0,2,1,5,4,3:T(8,128)(2,1)}), bf16[128,2,8,2,16,2,256]{6,0,2,1,5,4,3:T(8,128)(2,1)}) %all-gather.3.cloned.1.call-update) | async-done | bytes 67108880 | tf_op jit(solution)/shard_map/all_gather | solution.py:97
  1347.9 30.8 %reduce_sum.21 = bf16[32,2,8,2,16,2,256]{6,0,2,1,5,4,3:T(8,128)(2,1)} reduce(bf16[4,32,2,8,2,16,2,256]{7,1,0,3,2,6,5,4:T(8,128)(2,1)} %bitcast.30, bf16[]{:T(256)} %constant.30.clone.1), dimensions={0}, to_apply=%region_0.1 | reduce | flops 25165824 | bytes 83886080 | tf_op jit(solution)/shard_map/reduce_sum | solution.py:97
  1378.7 212.6 %copy.17 = bf16[32,2,8,2,16,2,256]{4,0,5,6,2,3,1:T(8,128)(2,1)} copy(bf16[32,2,8,2,16,2,256]{6,0,2,1,5,4,3:T(8,128)(2,1)} %reduce_sum.21) | data formatting | bytes 33554432 | tf_op jit(solution)/shard_map/reduce_sum | solution.py:97
  1591.3 44.7 %fusion = f32[32,8,2]{0,2,1:T(2,128)S(1)} fusion(bf16[32,2,8,2,16,2,256]{4,0,5,6,2,3,1:T(8,128)(2,1)} %copy.17), kind=kLoop, calls=%fused_computation.2 | loop fusion | flops 25165312 | bytes 16779264 | tf_op jit(solution)/shard_map/reduce_sum | solution.py:26
  1636.1 10.0 psum.7
  1646.1 88.3 %fusion.1 = bf16[32,2,8,2,16,2,256]{4,0,5,6,2,3,1:T(8,128)(2,1)} fusion(bf16[32,2,8,2,16,2,256]{4,0,5,6,2,3,1:T(8,128)(2,1)} %copy.17, f32[32,8,2]{0,2,1:T(2,128)S(1)} %add_rsqrt_fusion), kind=kLoop, calls=%fused_computation.3 | loop fusion | flops 25165824 | bytes 33556480 | tf_op jit(solution)/shard_map/convert_element_type | solution.py:31
  1734.4 94.8 %fusion.3 = f32[2,8,256,32,2,8,2]{3,5,6,4,2,1,0:T(8,128)} fusion(bf16[32,2,8,2,16,2,256]{4,0,5,6,2,3,1:T(8,128)(2,1)} %fusion.1, s32[]{:T(128)S(6)} %select_n.17), kind=kOutput, calls=%fused_computation.9 | convolution fusion | flops 134217728 | bytes 100663296 | tf_op jit(solution)/shard_map/sbcfpk,tbcfqk->cstbpqk/dot_general | solution.py:39
  1829.1 94.8 %fusion.2 = f32[2,8,256,32,2,8,2]{3,5,6,4,2,1,0:T(8,128)} fusion(bf16[32,2,8,2,16,2,256]{4,0,5,6,2,3,1:T(8,128)(2,1)} %fusion.1, s32[]{:T(128)S(6)} %select_n.17, s32[]{:T(128)S(6)} %add.99), kind=kOutput, calls=%fused_computation.8 | convolution fusion | flops 134217728 | bytes 100663304 | tf_op jit(solution)/shard_map/sbcfpk,tbcfqk->cstbpqk/dot_general | solution.py:39
  1923.9 97.4 %subtract_bitcast_fusion = f32[1,1,2,8,32,8,2,2,256]{4,3,6,7,8,5,2,1,0:T(8,128)} fusion(f32[2,8,256,32,2,8,2]{3,5,6,4,2,1,0:T(8,128)} %fusion.2, bf16[32,2,8,2,16,2,256]{4,0,5,6,2,3,1:T(8,128)(2,1)} %fusion.1, s32[]{:T(128)S(6)} %select_n.17), kind=kOutput, calls=%fused_computation.6 | convolution fusion | flops 138412032 | bytes 167772160 | tf_op jit(solution)/shard_map/sbcfpk,tbcfqk->cstbpqk/dot_general | solution.py:39
  2021.3 34.7 %copy.23 = f32[1,1,2,8,32,8,2,2,256]{8,5,7,6,4,3,2,1,0:T(8,128)} copy(f32[1,1,2,8,32,8,2,2,256]{4,3,6,7,8,5,2,1,0:T(8,128)} %subtract_bitcast_fusion) | data formatting | bytes 33554432 | tf_op jit(solution)/shard_map/stack | solution.py:49
  2056.0 97.2 %add_bitcast_fusion = f32[1,1,2,8,32,8,2,2,256]{4,3,6,7,8,5,2,1,0:T(8,128)} fusion(f32[2,8,256,32,2,8,2]{3,5,6,4,2,1,0:T(8,128)} %fusion.3, bf16[32,2,8,2,16,2,256]{4,0,5,6,2,3,1:T(8,128)(2,1)} %fusion.1, s32[]{:T(128)S(6)} %select_n.17, s32[]{:T(128)S(6)} %add.99), kind=kOutput, calls=%fused_computation.7 | convolution fusion | flops 138412032 | bytes 167772160 | tf_op jit(solution)/shard_map/sbcfpk,tbcfqk->cstbpqk/dot_general | solution.py:39
  2153.2 34.8 %copy.22 = f32[1,1,2,8,32,8,2,2,256]{8,5,7,6,4,3,2,1,0:T(8,128)} copy(f32[1,1,2,8,32,8,2,2,256]{4,3,6,7,8,5,2,1,0:T(8,128)} %add_bitcast_fusion) | data formatting | bytes 33554432 | tf_op jit(solution)/shard_map/stack | solution.py:49
  2188.0 24.9 %maximum_multiply_fusion = f32[1,2,2,8,32,8,2,2,256]{8,5,7,6,4,3,2,1,0:T(8,128)} fusion(f32[1,1,2,8,32,8,2,2,256]{8,5,7,6,4,3,2,1,0:T(8,128)} %copy.23, f32[1,1,2,8,32,8,2,2,256]{8,5,7,6,4,3,2,1,0:T(8,128)} %copy.22), kind=kLoop, calls=%fused_computation.12 | loop fusion | flops 16777216 | bytes 67108864 | tf_op jit(solution)/shard_map/div | solution.py:49
  2212.9 0.0 copy-start.1
  2212.9 46.3 %copy.24 = f32[1,2,2,8,32,8,2,2,256]{8,7,6,5,4,3,2,1,0:T(2,128)} copy(f32[1,2,2,8,32,8,2,2,256]{8,5,7,6,4,3,2,1,0:T(8,128)} %maximum_multiply_fusion) | data formatting | bytes 67108864 | tf_op jit(solution)/shard_map/div | solution.py:49
  2259.2 0.0 copy-done.1
  (6 shorter events, 0.0 us)
Async XLA Ops:
  6.5 12.4 copy-start
  6.5 1341.4 %all-gather.3.cloned.1.call-start = ((), (), s32[]{:S(2)}) async-start(), calls=%async_computation | async-start | bytes 83886080 | tf_op jit(solution)/shard_map/all_gather | solution.py:97
  6.5 28.2 %slice-start = ((s8[8388608]{0:T(1024)(128)(4,1)}), s8[4194304]{0:T(1024)(128)(4,1)S(1)}, s32[]{:S(2)}) async-start(s8[8388608]{0:T(1024)(128)(4,1)} %bitcast.122), calls=%async_computation.1 | async-start | bytes 8388608
  13.5 14.6 collective-permute-start
  19.7 15.1 slice-start.1
  176.1 4.5 copy-start.3
  197.8 7.8 copy-start.2
  2212.9 46.3 %copy-start.1 = (bf16[2,16,2,8]{1,3,2,0:T(8,128)(2,1)S(1)}, bf16[2,16,2,8]{1,3,2,0:T(8,128)(2,1)}, u32[]{:S(2)}) copy-start(bf16[2,16,2,8]{1,3,2,0:T(8,128)(2,1)} %param.9) | copy-start | bytes 3076
Sparse Core Ops, SparseCore 0:
  235.2 1112.6 all-gather.2
